TPU v7x, 32 devices: a whole 2x2x4 slice. The times are simulated.
32 devices in a mesh: dp: 8 (over z, x), tp: 4 (over y, core).
Axes of the slice: x: 2, y: 2, z: 4, core: 2. Of those that a mesh axis runs over, the one named last changes fastest.
Arguments:
- slopes: bfloat16 [8, 2, 3072, 768], P('dp', None, 'tp'), may hold values from -6 to 6, as said below
- basis_in: float32 [2, 768, 8], replicated, may hold values from -6 to 6
- weights_in: float32 [2, 3072, 768], P(None, 'tp', 'dp'), may hold values from -0.21875 to 0.21875
Outputs:
- new_weights: float32 [2, 3072, 768], P(None, 'tp', 'dp')
- new_basis: float32 [2, 768, 8], replicated
Inputs may be any that keep to these rules, and one draw needn't show every extreme that they name: slopes holds numbers from -6 to 6.
All inputs are finite; a program needn't handle non-finite values.
Results may differ from a plain program's by a relative error of at most 0.0003.
Values sent between devices are 32-bit elements.
A program may use at most 64 MiB of HBM per device.

v0:
```python
import jax
import jax.numpy as jnp
from jax import lax
from jax.sharding import PartitionSpec as P

RANK = 8


def body(slopes, basis_in, weights_in):
    own_grads = slopes[0]
    part_left = jnp.einsum(
        "liw,lwr->lir", own_grads, basis_in.astype(jnp.bfloat16), preferred_element_type=jnp.float32
    )
    left = lax.psum(part_left, "dp")
    part_gram = jnp.einsum("lir,lis->lrs", left, left, precision=lax.Precision.HIGHEST)
    small_left = left.astype(jnp.bfloat16)
    part_right = jnp.einsum(
        "liw,lir->lwr", own_grads, small_left, preferred_element_type=jnp.float32
    )
    own_share = part_gram / lax.axis_size("dp")
    right, gram = lax.psum((part_right, own_share), ("dp", "tp"))
    gram = gram + 0.001 * jnp.mean(jnp.diagonal(gram, axis1=1, axis2=2), axis=1)[
        :, None, None
    ] * jnp.eye(RANK, dtype=jnp.float32)
    place = lax.axis_index("dp") * weights_in.shape[2]
    own_right = lax.dynamic_slice_in_dim(right, place, weights_in.shape[2], axis=1)
    root = jnp.linalg.cholesky(gram)
    half = lax.linalg.triangular_solve(
        root, jnp.swapaxes(own_right, 1, 2), left_side=True, lower=True
    )
    mixed = lax.linalg.triangular_solve(root, half, left_side=True, lower=True, transpose_a=True)
    change = jnp.einsum(
        "lir,lrw->liw", left, mixed, precision=lax.Precision.HIGHEST
    ) / lax.axis_size("dp")
    new_weights = weights_in - 0.02 * change
    new_basis = right * lax.rsqrt(jnp.mean(right * right, axis=(1, 2), keepdims=True) + 1e-12)
    return (new_weights, new_basis)


def solution(mesh):
    placed = (P("dp", None, "tp", None), P(), P(None, "tp", "dp"))
    return jax.shard_map(
        body, mesh=mesh, in_specs=placed, out_specs=(P(None, "tp", "dp"), P()), check_vma=False
    )
```

profile of v0, /device:TPU:0, one launch (start us, length us, event | category | flops | bytes accessed | tf_op | source)
XLA Modules:
  0.0 87.7 jit_solution(12999612383202632761)
XLA Ops:
  0.6 0.0 copy-start
  0.7 0.1 copy.11
  0.8 1.5 %copy-done = bf16[1,2,768,768]{3,2,1,0:T(8,128)(2,1)S(1)} copy-done((bf16[1,2,768,768]{3,2,1,0:T(8,128)(2,1)S(1)}, bf16[1,2,768,768]{3,2,1,0:T(8,128)(2,1)}, u32[]{:S(2)}) %copy-start) | copy-done | bytes 2359320
  2.3 0.0 copy-start.1
  2.3 1.6 %fusion.2 = f32[2,768,8]{1,2,0:T(8,128)S(1)} fusion(bf16[1,2,768,768]{3,2,1,0:T(8,128)(2,1)S(1)} %copy-done, f32[2,768,8]{1,2,0:T(8,128)} %param.4), kind=kOutput, calls=%fused_computation.3 | convolution fusion | flops 18886656 | bytes 2457600 | tf_op jit(solution)/shard_map/liw,lwr->lir/dot_general | solution.py:11
  3.9 39.3 %psum.21 = f32[2,768,8]{1,2,0:T(8,128)S(1)} all-reduce(f32[2,768,8]{1,2,0:T(8,128)S(1)} %fusion.2), channel_id=1, replica_groups=mesh['dp'=8,'tp'=4] {'dp'}, use_global_device_ids=true, to_apply=%region_0.0 | all-reduce | flops 12288 | bytes 98304 | tf_op jit(solution)/shard_map/psum | solution.py:14
  43.2 0.2 convolution_multiply_fusion.1
  43.4 0.4 fusion.5
  43.8 37.3 %all-reduce = (f32[2,8,8]{1,2,0:T(8,128)S(1)}, f32[2,768,8]{1,2,0:T(8,128)S(1)}) all-reduce(f32[2,8,8]{1,2,0:T(8,128)S(1)} %convolution_multiply_fusion.1, f32[2,768,8]{1,2,0:T(8,128)S(1)} %fusion.5), channel_id=1, replica_groups=mesh['dp'=8,'tp'=4] {'dp','tp'}, use_global_device_ids=true, to_apply=%region_1.0 | all-reduce | flops 12416 | bytes 99328 | tf_op jit(solution)/shard_map/psum | solution.py:21
  81.2 0.1 multiply_reduce_fusion
  81.3 0.1 copy.13
  81.4 0.6 gather_fusion
  82.0 0.1 multiply_add_fusion
  82.1 0.1 copy.14
  82.2 0.1 fusion.14
  82.2 1.4 %custom-call.9 = f32[2,8,8]{2,1,0:T(8,128)S(1)} custom-call(f32[2,8,8]{2,1,0:T(8,128)S(1)} %fusion.14), custom_call_target="Cholesky" | custom-call | tf_op jit(solution)/shard_map/jit(cholesky)/cholesky | solution.py:27
  83.7 0.1 select_reduce_fusion
  83.7 0.1 compare_reduce_fusion
  83.9 0.1 select_bitcast_fusion
  83.9 1.3 %custom-call.10 = f32[2,1,8,8]{2,3,1,0:T(8,128)S(1)} custom-call(f32[2,1,8,8]{3,2,1,0:T(8,128)S(1)} %select_bitcast_fusion), custom_call_target="InvertDiagBlocksLowerTriangular" | custom-call | tf_op jit(solution)/shard_map/triangular_solve | solution.py:31
  85.2 0.2 fusion.10
  85.4 0.1 fusion.12
  85.6 0.7 broadcast_multiply_fusion
  86.3 0.0 copy-done.1
  86.3 1.5 %fusion.4 = f32[2,768,96]{1,2,0:T(8,128)} fusion(f32[2,768,96]{1,2,0:T(8,128)S(1)} %copy-done.1, f32[2,768,8]{1,2,0:T(8,128)S(1)} %psum.21, f32[2,8,96]{2,1,0:T(8,128)S(1)} %fusion.12), kind=kOutput, calls=%fused_computation.6 | convolution fusion | flops 14450688 | bytes 1234944 | tf_op jit(solution)/shard_map/lir,lrw->liw/dot_general | solution.py:32
  (7 shorter events, 0.1 us)
Async XLA Ops:
  0.6 1.7 %copy-start = (bf16[1,2,768,768]{3,2,1,0:T(8,128)(2,1)S(1)}, bf16[1,2,768,768]{3,2,1,0:T(8,128)(2,1)}, u32[]{:S(2)}) copy-start(bf16[1,2,768,768]{3,2,1,0:T(8,128)(2,1)} %param.3) | copy-start | bytes 7077892
  2.3 84.0 %copy-start.1 = (f32[2,768,96]{1,2,0:T(8,128)S(1)}, f32[2,768,96]{1,2,0:T(8,128)}, u32[]{:S(2)}) copy-start(f32[2,768,96]{1,2,0:T(8,128)} %param.5) | copy-start | bytes 1769476
where the time goes:
time: 88.6 us; the launch traced here: 87.7 us
  blocking collectives  76.7 us (87%)
  matrix products  4.02 us (5%)
  other arithmetic  3.96 us (4%)
  local copies, waits for them, and re-layouts  2.39 us (3%)
    psum x1, blocking collectives, body(): left = lax.psum(part_left, 'dp')  39.3 us
    psum x1, blocking collectives, body(): right, gram = lax.psum((part_right, own_share), ('dp', 'tp'))  37.3 us

commit v1 on v0

v1 whole, which is shorter than its diff:
```python
import functools

import jax
import jax.numpy as jnp
from jax import lax
from jax.experimental import pallas as pl
from jax.experimental.pallas import tpu as pltpu
from jax.sharding import PartitionSpec as P

MESH = pl.DeviceIdType.MESH
HIGH = lax.Precision.HIGHEST
LANES = 128


def dot(a, b, dims, precision=None):
    return lax.dot_general(
        a, b, ((dims[:1], dims[1:]), ((), ())), precision=precision, preferred_element_type=jnp.float32
    )


def split(x):
    parts = []
    for _ in range(3):
        part = x.astype(jnp.bfloat16).astype(jnp.float32)
        parts.append(part)
        x = x - part
    return parts


def stack(x, order):
    parts = split(x)
    return jnp.concatenate([parts[k] for k in order], axis=0).astype(jnp.bfloat16)


LEFT_ORDER = (0, 0, 1, 0, 2, 1)
RIGHT_ORDER = (0, 1, 0, 2, 0, 1)


def kernel(
    n, m, layers, rank, slopes_ref, basis_ref, weights_ref, out_ref, basis_out_ref,
    slopes, weights, part1, got1, all1, left_ref, part2, got2, tp2, all2, grams,
    in_sem, w_sem, o_sem, s1, r1, s2, r2, s3, r3, s4, r4, s5, r5, s6, r6,
):
    dp = lax.axis_index("dp")
    tp = lax.axis_index("tp")
    dp_peer = [None] + [lax.rem(dp + k, n) for k in range(1, n)]
    tp_peer = [None] + [lax.rem(tp + k, m) for k in range(1, m)]
    rows_all = layers * rank
    depth = slopes.shape[1]
    block = out_ref.shape[1]
    rows, lanes = part1.shape[1:]
    per_row = depth // lanes

    loads = []
    for l in range(layers):
        copy = pltpu.make_async_copy(slopes_ref.at[l], slopes.at[l], in_sem.at[l])
        copy.start()
        loads.append(copy)
    w_load = pltpu.make_async_copy(weights_ref, weights, w_sem)
    w_load.start()

    barrier = pltpu.get_barrier_semaphore()
    for k in range(1, n):
        pl.semaphore_signal(barrier, inc=1, device_id=(dp_peer[k], tp), device_id_type=MESH)
    for k in range(1, m):
        pl.semaphore_signal(barrier, inc=1, device_id=(dp, tp_peer[k]), device_id_type=MESH)

    def dp_copy(src, dst, k, send, recv):
        return pltpu.make_async_remote_copy(
            src_ref=src, dst_ref=dst, send_sem=send.at[k], recv_sem=recv.at[k],
            device_id=(dp_peer[k], tp), device_id_type=MESH,
        )

    def tp_copy(src, dst, k, send, recv):
        return pltpu.make_async_remote_copy(
            src_ref=src, dst_ref=dst, send_sem=send.at[k], recv_sem=recv.at[k],
            device_id=(dp, tp_peer[k]), device_id_type=MESH,
        )

    def place(c):
        row = c // per_row * rows
        lane = c % per_row * lanes
        return slice(row, row + rows), slice(lane, lane + lanes)

    for l in range(layers):
        loads[l].wait()
        left_ref[l * rank:(l + 1) * rank, :] = dot(
            basis_ref[l].astype(jnp.bfloat16), slopes[l], (1, 1)
        )
    for c in range(n):
        at = place(c)
        part1[c] = left_ref[at[0], at[1]]
    pl.semaphore_wait(barrier, n + m - 2)

    sends = [dp_copy(part1.at[dp_peer[k]], got1.at[k], k, s1, r1) for k in range(1, n)]
    for copy in sends:
        copy.start()
    total = part1[dp]
    for k in range(1, n):
        sends[k - 1].wait_recv()
        total = total + got1[k]
    all1[dp] = total
    gathers = [dp_copy(all1.at[dp], all1.at[dp], k, s2, r2) for k in range(1, n)]
    for copy in gathers:
        copy.start()
    for copy in sends:
        copy.wait_send()
    for copy in gathers:
        copy.wait_recv()
    for c in range(n):
        at = place(c)
        left_ref[at[0], at[1]] = all1[c]
    lefts = [left_ref[l * rank:(l + 1) * rank, :] for l in range(layers)]

    for l in range(layers):
        term = dot(lefts[l].astype(jnp.bfloat16), slopes[l], (1, 0))
        for c in range(n):
            part2[c, l * rank:(l + 1) * rank, :] = jnp.concatenate(
                [term[:, c * block:(c + 1) * block], jnp.zeros((rank, LANES - block), jnp.float32)], axis=1
            )
    sends2 = [dp_copy(part2.at[dp_peer[k]], got2.at[k], k, s3, r3) for k in range(1, n)]
    for copy in sends2:
        copy.start()

    own = [dot(left, left, (1, 1), HIGH) for left in lefts]
    grams[tp] = jnp.concatenate(
        own + [jnp.zeros((rank, LANES - layers * rank), jnp.float32)], axis=1
    )
    gram_sends = [tp_copy(grams.at[tp], grams.at[tp], k, s5, r5) for k in range(1, m)]
    for copy in gram_sends:
        copy.start()
    for copy in gathers:
        copy.wait_send()
    for copy in gram_sends:
        copy.wait_recv()
    gram_all = grams[0]
    for k in range(1, m):
        gram_all = gram_all + grams[k]
    row_id = lax.broadcasted_iota(jnp.int32, (rank, rank), 0)
    col_id = lax.broadcasted_iota(jnp.int32, (rank, rank), 1)
    eye = (row_id == col_id).astype(jnp.float32)
    wide_row = lax.broadcasted_iota(jnp.int32, (rank, 2 * rank), 0)
    tables = []
    for l in range(layers):
        gram = gram_all[:, l * rank:(l + 1) * rank]
        mean = jnp.sum(gram * eye, keepdims=True) / rank
        tables.append(jnp.concatenate([gram + 0.001 * mean * eye, eye], axis=1))
    for step in range(rank - 1):
        for l in range(layers):
            table = tables[l]
            factor = table[:, step:step + 1] / table[step:step + 1, step:step + 1]
            change = factor * table[step:step + 1, :]
            tables[l] = table - jnp.where(wide_row > step, change, 0.0)
    solved = []
    for l in range(layers):
        lower = tables[l][:, rank:]
        pivots = jnp.sum(tables[l][:, :rank] * eye, axis=1, keepdims=True)
        half = dot(lower, lefts[l], (1, 0), HIGH) / pivots
        full = dot(lower, half, (0, 0), HIGH) * (0.02 / n)
        solved.append(stack(full, LEFT_ORDER))

    total = part2[dp]
    for k in range(1, n):
        sends2[k - 1].wait_recv()
        total = total + got2[k]
    tp2[tp] = total
    tp_sends = [tp_copy(tp2.at[tp], tp2.at[tp], k, s4, r4) for k in range(1, m)]
    for copy in tp_sends:
        copy.start()
    for copy in sends2:
        copy.wait_send()
    for copy in tp_sends:
        copy.wait_recv()
    total = tp2[0]
    for k in range(1, m):
        total = total + tp2[k]
    all2[dp] = total
    gathers2 = [dp_copy(all2.at[dp], all2.at[dp], k, s6, r6) for k in range(1, n)]
    for copy in gathers2:
        copy.start()

    w_load.wait()
    outs = []
    for l in range(layers):
        mine = stack(total[l * rank:(l + 1) * rank, :], RIGHT_ORDER)
        change = dot(mine, solved[l], (0, 0))
        weights[l] = weights[l] - change[:block, :]
        copy = pltpu.make_async_copy(weights.at[l], out_ref.at[l], o_sem.at[l])
        copy.start()
        outs.append(copy)

    for copy in gram_sends + tp_sends:
        copy.wait_send()
    for copy in gathers2:
        copy.wait_recv()
    for l in range(layers):
        pieces = [all2[c, l * rank:(l + 1) * rank, :] for c in range(n)]
        square = pieces[0] * pieces[0]
        for piece in pieces[1:]:
            square = square + piece * piece
        mean = jnp.sum(square, keepdims=True) / (rank * n * block)
        scale = lax.rsqrt(mean + 1e-12)
        for c in range(n):
            basis_out_ref[l, :, c * block:(c + 1) * block] = (pieces[c] * scale)[:, :block]
    for copy in gathers2:
        copy.wait_send()
    for copy in outs:
        copy.wait()


def body(slopes, basis_in, weights_in):
    n = lax.axis_size("dp")
    m = lax.axis_size("tp")
    _, layers, depth, width = slopes.shape
    rank = basis_in.shape[2]
    block = weights_in.shape[2]
    total = layers * rank
    rows = max(1, total // n)
    lanes = total * depth // (n * rows)
    f32 = jnp.float32
    dma = pltpu.SemaphoreType.DMA
    any_spec = pl.BlockSpec(memory_space=pl.ANY)
    vmem_spec = pl.BlockSpec(memory_space=pltpu.VMEM)
    new_weights, new_basis = pl.pallas_call(
        functools.partial(kernel, n, m, layers, rank),
        out_shape=(
            jax.ShapeDtypeStruct((layers, block, depth), f32),
            jax.ShapeDtypeStruct((layers, rank, width), f32),
        ),
        in_specs=[any_spec, vmem_spec, any_spec],
        out_specs=(any_spec, vmem_spec),
        scratch_shapes=[
            pltpu.VMEM((layers, depth, width), jnp.bfloat16),
            pltpu.VMEM((layers, block, depth), f32),
            pltpu.VMEM((n, rows, lanes), f32),
            pltpu.VMEM((n, rows, lanes), f32),
            pltpu.VMEM((n, rows, lanes), f32),
            pltpu.VMEM((total, depth), f32),
            pltpu.VMEM((n, total, LANES), f32),
            pltpu.VMEM((n, total, LANES), f32),
            pltpu.VMEM((m, total, LANES), f32),
            pltpu.VMEM((n, total, LANES), f32),
            pltpu.VMEM((m, rank, LANES), f32),
            dma((layers,)), dma, dma((layers,)),
            dma((n,)), dma((n,)), dma((n,)), dma((n,)), dma((n,)), dma((n,)),
            dma((m,)), dma((m,)), dma((m,)), dma((m,)), dma((n,)), dma((n,)),
        ],
        compiler_params=pltpu.CompilerParams(collective_id=0, has_side_effects=True),
    )(slopes[0], jnp.swapaxes(basis_in, 1, 2), jnp.swapaxes(weights_in, 1, 2))
    return jnp.swapaxes(new_weights, 1, 2), jnp.swapaxes(new_basis, 1, 2)


def solution(mesh):
    placed = (P("dp", None, "tp", None), P(), P(None, "tp", "dp"))
    return jax.shard_map(
        body, mesh=mesh, in_specs=placed, out_specs=(P(None, "tp", "dp"), P()), check_vma=False
    )
```

time: 88.6 us -> 33.1 us (0.37)
  blocking collectives: 76.7 us -> 0 us
  Pallas kernels: 0 us -> 28.8 us
  matrix products: 4.02 us -> 0 us
  other arithmetic: 3.96 us -> 0 us
  local copies, waits for them, and re-layouts: 2.39 us -> 3.34 us
    psum x2 -> x0, blocking collectives: 76.7 us -> none  [the longest x1 39.3 us: body(): left = lax.psum(part_left, 'dp')]
    pallas_call x0 -> x1, Pallas kernels: none -> 28.8 us  [body(): pl.pallas_call(functools.partial(kernel, n, m, layers, rank), out_shape=(...]
    dot_general x4 -> x0, matrix products: 3.64 us -> none  [the longest x1 1.56 us: body(): jnp.einsum('liw,lwr->lir', own_grads, basis_in.astype(jnp.bfloat16), pref...]
    another operation x7 -> x0, other arithmetic: 2.95 us -> none  [the longest x4 1.61 us: body(): root = jnp.linalg.cholesky(gram)]
    unnamed x4 -> x2, local copies, waits for them, and re-layouts: 1.53 us -> 3.34 us
where the time goes in v1:
time: 33.1 us; the launch traced here: 32.8 us
  Pallas kernels  28.8 us (87%)
  local copies, waits for them, and re-layouts  3.34 us (10%)
  between operations  0.64 us (2%)
    pallas_call x1, Pallas kernels, body(): pl.pallas_call(functools.partial(kernel, n, m, layers, rank), out_shape=(...  28.8 us
    unnamed x2, local copies, waits for them, and re-layouts  3.34 us

profile of v1, /device:TPU:0, one launch (start us, length us, event | category | flops | bytes accessed | tf_op | source)
XLA Modules:
  0.0 32.8 jit_solution(11047607667756374454)
XLA Ops:
  0.6 28.8 %shard_map.50 = (f32[2,96,768]{2,1,0:T(8,128)}, f32[2,8,768]{2,1,0:T(8,128)}) custom-call(bf16[2,768,768]{2,1,0:T(8,128)(2,1)} %bitcast.5, f32[2,8,768]{2,1,0:T(8,128)} %bitcast.9, f32[2,96,768]{2,1,0:T(8,128)} %bitcast.7), custom_call_target="tpu_custom_call" | custom-call | tf_op jit(solution)/shard_map/pallas_call | solution.py:224
  29.4 1.9 %copy.7 = f32[2,768,96]{1,2,0:T(8,128)} copy(f32[2,768,96]{1,2,0:T(8,128)} %bitcast.6) | data formatting | bytes 1179648
  31.4 1.4 %copy.8 = f32[2,768,8]{1,2,0:T(8,128)} copy(f32[2,768,8]{1,2,0:T(8,128)} %bitcast.8) | data formatting | bytes 98304
